TPU v7x, 32 devices: a whole 2x2x4 slice. The times are simulated.
32 devices in a mesh: path: 16 (over z, x, core), shard: 2 (over y).
Axes of the slice: x: 2, y: 2, z: 4, core: 2. Of those that a mesh axis runs over, the one named last changes fastest.
Arguments:
- deltas: bfloat16 [16, 32, 4096], P('path', 'shard'), may hold values from -96 to 96
- momentum: float32 [16, 32, 4096], P(None, 'shard', 'path'), may hold values from -4 to 4
- path_module: int32 [16], replicated, may hold values from 0 to 15, as said below
Outputs:
- path_update: bfloat16 [16, 32, 4096], P('path', 'shard')
- new_momentum: float32 [16, 32, 4096], P(None, 'shard', 'path')
Inputs may be any that keep to these rules, and one draw needn't show every extreme that they name: `path_module`: every module is used by at least one and at most seven paths.
All inputs are finite; a program needn't handle non-finite values.
Results may differ from a plain program's by a relative error of at most 0.0004.
Values may be sent and summed in bfloat16 or wider, within the bound.
A program may use at most 64 MiB of HBM per device.

v0:
```python
import functools
import math

import jax
import jax.numpy as jnp
from jax import lax
from jax.experimental import pallas as pl
from jax.experimental.pallas import tpu as pltpu
from jax.sharding import PartitionSpec as P

outer_rate = 0.7
momentum_rate = 0.9
clip_ratio = 2.0
LANES = 128
MESH = pl.DeviceIdType.MESH


def kernel(
    n,
    s,
    deltas_ref,
    momentum_ref,
    path_module_ref,
    update,
    new,
    module_ref,
    own,
    pieces,
    momentum,
    grad,
    step,
    chosen,
    mine,
    squares,
    load_sem,
    send_sem,
    recv_sem,
    square_send,
    square_recv,
    back_send,
    back_recv,
):
    me, my_shard = lax.axis_index("path"), lax.axis_index("shard")
    modules, rows, columns = momentum.shape
    width = own.shape[1]
    everyone = [(k, j) for k in range(n) for j in range(s) if (k, j) != (0, 0)]

    def peer(k, j=0):
        there, shard = me + k, my_shard + j
        return jnp.where(there < n, there, there - n), jnp.where(shard < s, shard, shard - s)

    def device(k, j=0):
        there, shard = peer(k, j)
        return {"path": there, "shard": shard}

    def arrived(buffer, sem):
        pltpu.make_async_copy(buffer, buffer, sem).wait()

    def targets():
        size = math.gcd(n, 4)
        groups = n // size
        group, place = me // size, lax.rem(me, size)
        low = group < groups // 2
        for a in range(groups):
            down, up = groups - 1 - a, a
            down = jnp.where(down <= group, down - 1, down)
            up = jnp.where(up >= group, up + 1, up)
            other = group if a == groups - 1 else jnp.where(low, down, up)
            for b in range(1 if a == groups - 1 else 0, size):
                at = place + b
                yield other * size + jnp.where(at < size, at, at - size)

    def block(index):
        return pl.ds(pl.multiple_of(index * columns, columns), columns)

    barrier = pltpu.get_barrier_semaphore()
    for k, j in everyone:
        pl.semaphore_signal(barrier, inc=1, device_id=device(k, j), device_id_type=MESH)
    load_module = pltpu.make_async_copy(path_module_ref, module_ref, load_sem.at[2])
    load_module.start()
    load_own = pltpu.make_async_copy(deltas_ref.at[0], own, load_sem.at[0])
    load_own.start()
    load_momentum = pltpu.make_async_copy(momentum_ref, momentum, load_sem.at[1])
    load_momentum.start()
    load_module.wait()

    lane = lax.broadcasted_iota(jnp.int32, (1, n * rows), 1)
    target = jnp.zeros((1, n * rows), jnp.int32)
    for p in range(n):
        inside = (lane >= p * rows) & (lane < (p + 1) * rows)
        target = jnp.where(inside, lane + (module_ref[p] - p) * rows, target)
    row = lax.broadcasted_iota(jnp.int32, (modules * rows, n * rows), 0)
    spread = (row == target).astype(jnp.float32)
    scale = 1.0 / jnp.sum(spread, axis=1, keepdims=True)
    spread = spread.astype(jnp.bfloat16)

    load_own.wait()
    keep_own = pltpu.make_async_copy(own.at[:, block(me)], pieces.at[me], recv_sem)
    keep_own.start()
    pl.semaphore_wait(barrier, len(everyone))
    for there in targets():
        copy = pltpu.make_async_remote_copy(
            src_ref=own.at[:, block(there)],
            dst_ref=pieces.at[me],
            send_sem=send_sem,
            recv_sem=recv_sem,
            device_id={"path": there, "shard": my_shard},
            device_id_type=MESH,
        )
        copy.start()
    arrived(pieces, recv_sem)

    total = jnp.dot(
        spread, pieces[...].reshape(n * rows, columns), preferred_element_type=jnp.float32
    )
    outer_grad = (total * scale).reshape(modules, rows, columns)
    grad[...] = outer_grad
    by_row = jnp.sum(outer_grad * outer_grad, axis=1)
    by_module = jnp.sum(by_row, axis=1, keepdims=True)
    on_diagonal = lax.broadcasted_iota(
        jnp.int32, (modules, LANES), 0
    ) == lax.broadcasted_iota(jnp.int32, (modules, LANES), 1)
    own_squares = jnp.sum(jnp.where(on_diagonal, by_module, 0.0), axis=0, keepdims=True)
    my_slot = me * s + my_shard
    mine[...] = own_squares
    for k, j in everyone:
        copy = pltpu.make_async_remote_copy(
            src_ref=mine,
            dst_ref=squares.at[my_slot],
            send_sem=square_send,
            recv_sem=square_recv,
            device_id=device(k, j),
            device_id_type=MESH,
        )
        copy.start()
    pltpu.make_async_copy(mine, squares.at[my_slot], square_recv).start()
    load_momentum.wait()
    arrived(squares, square_recv)
    norm_squares = jnp.sum(squares[...], axis=0)
    limit = clip_ratio * math.sqrt(rows * s * width)
    shrink = jnp.minimum(1.0, limit / jnp.sqrt(norm_squares + 1e-06))
    at_lane = lax.broadcasted_iota(jnp.int32, (1, LANES), 1)
    for m in range(modules):
        factor = jnp.sum(jnp.where(at_lane == m, shrink, 0.0), axis=1, keepdims=True)
        clipped = grad[m] * factor
        moved = momentum_rate * momentum[m] + clipped
        new[m] = moved
        step[m] = (outer_rate * (clipped + momentum_rate * moved)).astype(jnp.bfloat16)
    chosen[me] = step[module_ref[me]]
    for k in range(1, n):
        there, _ = peer(k)
        chosen[there] = step[module_ref[there]]
        copy = pltpu.make_async_remote_copy(
            src_ref=chosen.at[there],
            dst_ref=update.at[0, :, block(me)],
            send_sem=back_send,
            recv_sem=back_recv,
            device_id=device(k),
            device_id_type=MESH,
        )
        copy.start()
    pltpu.make_async_copy(
        chosen.at[me], update.at[0, :, block(me)], back_recv
    ).start()
    arrived(pieces.at[pl.ds(0, n - 1)], send_sem)
    arrived(squares.at[pl.ds(0, len(everyone))], square_send)
    arrived(chosen.at[pl.ds(0, n - 1)], back_send)
    arrived(update, back_recv)


def write(update, new, update_ref, new_ref, sem):
    copies = [
        pltpu.make_async_copy(update, update_ref, sem.at[0]),
        pltpu.make_async_copy(new, new_ref, sem.at[1]),
    ]
    for copy in copies:
        copy.start()
    for copy in copies:
        copy.wait()


def direct(n, s, deltas, momentum, path_module):
    modules, rows, columns = momentum.shape
    width = deltas.shape[2]
    dma = pltpu.SemaphoreType.DMA
    anywhere = pl.BlockSpec(memory_space=pl.ANY)
    in_vmem = pl.BlockSpec(memory_space=pltpu.VMEM)
    held = pl.pallas_call(
        functools.partial(kernel, n, s),
        out_shape=(
            pltpu.VMEM(deltas.shape, jnp.bfloat16),
            pltpu.VMEM(momentum.shape, jnp.float32),
        ),
        in_specs=[anywhere, anywhere, anywhere],
        out_specs=(in_vmem, in_vmem),
        scratch_shapes=[
            pltpu.SMEM(path_module.shape, jnp.int32),
            pltpu.VMEM((rows, width), jnp.bfloat16),
            pltpu.VMEM((n, rows, columns), jnp.bfloat16),
            pltpu.VMEM((modules, rows, columns), jnp.float32),
            pltpu.VMEM((modules, rows, columns), jnp.float32),
            pltpu.VMEM((modules, rows, columns), jnp.bfloat16),
            pltpu.VMEM((n, rows, columns), jnp.bfloat16),
            pltpu.VMEM((1, LANES), jnp.float32),
            pltpu.VMEM((n * s, 1, LANES), jnp.float32),
            dma((3,)),
            dma,
            dma,
            dma,
            dma,
            dma,
            dma,
        ],
        compiler_params=pltpu.CompilerParams(collective_id=0, has_side_effects=True),
    )(deltas, momentum, path_module)
    return pl.pallas_call(
        write,
        out_shape=(
            jax.ShapeDtypeStruct(deltas.shape, jnp.bfloat16),
            jax.ShapeDtypeStruct(momentum.shape, jnp.float32),
        ),
        in_specs=[in_vmem, in_vmem],
        out_specs=(anywhere, anywhere),
        scratch_shapes=[dma((2,))],
    )(*[pltpu.with_memory_space_constraint(x, pltpu.VMEM) for x in held])


def by_collectives(s, deltas, momentum, path_module):
    modules = momentum.shape[0]
    rows, width = deltas.shape[1:]
    onehot = path_module[:, None] == jnp.arange(modules, dtype=jnp.int32)[None, :]
    counts = jnp.sum(onehot.astype(jnp.float32), axis=0)
    pieces = lax.all_to_all(deltas, "path", split_axis=2, concat_axis=0, tiled=True)
    totals = jnp.einsum(
        "pm,prc->mrc", onehot.astype(jnp.bfloat16), pieces, preferred_element_type=jnp.float32
    )
    outer_grad = totals / counts[:, None, None]
    local_squares = jnp.sum(outer_grad * outer_grad, axis=(1, 2))
    norm_squares = lax.psum(local_squares, ("path", "shard"))
    limit = clip_ratio * math.sqrt(rows * s * width)
    shrink = jnp.minimum(1.0, limit / jnp.sqrt(norm_squares + 1e-06))
    clipped = outer_grad * shrink[:, None, None]
    new_momentum = momentum_rate * momentum + clipped
    outer_step = (outer_rate * (clipped + momentum_rate * new_momentum)).astype(jnp.bfloat16)
    chosen = jnp.take(outer_step, path_module, axis=0)
    path_update = lax.all_to_all(chosen, "path", split_axis=0, concat_axis=2, tiled=True)
    return (path_update, new_momentum)


def local(n, s, deltas, momentum, path_module):
    modules, rows, columns = momentum.shape
    aligned = columns % LANES == 0 and rows % 16 == 0 and modules <= LANES
    if aligned and n > 1:
        return direct(n, s, deltas, momentum, path_module)
    return by_collectives(s, deltas, momentum, path_module)


def solution(mesh):
    return jax.shard_map(
        functools.partial(local, mesh.shape["path"], mesh.shape["shard"]),
        mesh=mesh,
        in_specs=(P("path", "shard", None), P(None, "shard", "path"), P()),
        out_specs=(P("path", "shard", None), P(None, "shard", "path")),
        check_vma=False,
    )
```

profile of v0, /device:TPU:0, one launch (start us, length us, event | category | flops | bytes accessed | tf_op | source)
XLA Modules:
  0.0 21.0 jit_solution(7073615365743450334)
XLA Ops:
  0.6 19.6 %shard_map.50 = (bf16[1,16,4096]{2,1,0:T(8,128)(2,1)S(1)}, f32[16,16,256]{2,1,0:T(8,128)S(1)}) custom-call(bf16[1,16,4096]{2,1,0:T(8,128)(2,1)} %deltas_ref.1, f32[16,16,256]{2,1,0:T(8,128)} %momentum_ref.1, s32[16]{0:T(128)} %path_module_ref.1), custom_call_target="tpu_custom_call" | custom-call | tf_op jit(solution)/shard_map/pallas_call | solution.py:188
  20.2 0.8 %shard_map.51 = (bf16[1,16,4096]{2,1,0:T(8,128)(2,1)}, f32[16,16,256]{2,1,0:T(8,128)}) custom-call(bf16[1,16,4096]{2,1,0:T(8,128)(2,1)S(1)} %get-tuple-element.4.update, f32[16,16,256]{2,1,0:T(8,128)S(1)} %get-tuple-element.5.new), custom_call_target="tpu_custom_call" | custom-call | tf_op jit(solution)/shard_map/pallas_call | solution.py:216
where the time goes:
time: 21.1 us; the launch traced here: 21 us
  Pallas kernels  20.3 us (96%)
  between operations  0.64 us (3%)
    pallas_call x1, Pallas kernels, direct(): pl.pallas_call(functools.partial(kernel, n, s), out_shape=(pltpu.VMEM(del...  19.6 us
    pallas_call x1, Pallas kernels, direct(): pl.pallas_call(write, out_shape=(jax.ShapeDtypeStruct(deltas.shape, jnp.b...  0.77 us

commit v1 on v0

v1 whole, which is shorter than its diff:
```python
import functools
import math

import jax
import jax.numpy as jnp
from jax import lax
from jax.experimental import pallas as pl
from jax.experimental.pallas import tpu as pltpu
from jax.sharding import PartitionSpec as P

outer_rate = 0.7
momentum_rate = 0.9
clip_ratio = 2.0
LANES = 128
MESH = pl.DeviceIdType.MESH


def kernel(
    n,
    s,
    deltas_ref,
    momentum_ref,
    path_module_ref,
    update,
    new,
    module_ref,
    own,
    momentum,
    chosen,
    pieces,
    moments,
    mine,
    pair,
    total,
    squares,
    shrink,
    load_sem,
    ready,
    pair_ready,
    piece_send,
    piece_recv,
    moment_send,
    moment_recv,
    pair_send,
    pair_recv,
    square_send,
    square_recv,
):
    me, my_shard = lax.axis_index("path"), lax.axis_index("shard")
    modules, rows, columns = momentum.shape
    width = own.shape[1]
    size = math.gcd(n, 4)
    groups = n // size
    group, place = lax.div(me, size), lax.rem(me, size)

    def device(path, shard=my_shard):
        return {"path": path, "shard": shard}

    def arrived(buffer, sem):
        pltpu.make_async_copy(buffer, buffer, sem).wait()

    def wait_for(sem, signals):
        @pl.when(signals > 0)
        def _():
            pl.semaphore_wait(sem, signals)

    def block(index):
        return pl.ds(pl.multiple_of(index * columns, columns), columns)

    def push(path):
        pltpu.make_async_remote_copy(
            src_ref=own.at[:, block(path)],
            dst_ref=pieces.at[me],
            send_sem=piece_send,
            recv_sem=piece_recv,
            device_id=device(path),
            device_id_type=MESH,
        ).start()
        pltpu.make_async_remote_copy(
            src_ref=chosen.at[path],
            dst_ref=moments.at[me],
            send_sem=moment_send,
            recv_sem=moment_recv,
            device_id=device(path),
            device_id_type=MESH,
        ).start()

    barrier = pltpu.get_barrier_semaphore()
    for path in range(1, n):
        @pl.when(path > me)
        def _():
            pl.semaphore_signal(barrier, inc=1, device_id=device(path), device_id_type=MESH)
    for shard in range(1, s):
        @pl.when(shard > my_shard)
        def _():
            pl.semaphore_signal(barrier, inc=1, device_id=device(me, shard), device_id_type=MESH)

    load_module = pltpu.make_async_copy(path_module_ref, module_ref, load_sem.at[0])
    load_own = pltpu.make_async_copy(deltas_ref.at[0], own, load_sem.at[1])
    load_momentum = pltpu.make_async_copy(momentum_ref, momentum, load_sem.at[2])
    load_module.start()
    load_own.start()
    load_momentum.start()
    load_own.wait()
    load_module.wait()
    load_momentum.wait()
    for path in range(n):
        chosen[path] = momentum[module_ref[path]]

    wait_for(barrier, me + my_shard)
    for path in range(n - 1):
        @pl.when(path < me)
        def _():
            distance = group - path // size
            pl.semaphore_signal(ready.at[distance], inc=1, device_id=device(path), device_id_type=MESH)
    for shard in range(s - 1):
        @pl.when(shard < my_shard)
        def _():
            pl.semaphore_signal(pair_ready, inc=1, device_id=device(me, shard), device_id_type=MESH)
    for path in range(n - 1):
        @pl.when(path < me)
        def _():
            push(path)

    held = own[...].astype(jnp.float32)
    by_column = jnp.sum(held * held, axis=0, keepdims=True)
    mine[...] = jnp.broadcast_to(jnp.sum(by_column, axis=1, keepdims=True), mine.shape)
    pieces[me] = own[:, block(me)]
    moments[me] = chosen[me]

    wait_for(ready.at[0], size - 1 - place)
    for at in range(1, size):
        @pl.when(at > place)
        def _():
            push(group * size + at)
    wait_for(pair_ready, s - 1 - my_shard)
    for j in range(1, s):
        shard = lax.rem(my_shard + j, s)
        pltpu.make_async_remote_copy(
            src_ref=mine,
            dst_ref=pair.at[my_shard],
            send_sem=pair_send,
            recv_sem=pair_recv,
            device_id=device(me, shard),
            device_id_type=MESH,
        ).start()
    pair[my_shard] = mine[...]
    for distance in range(1, groups):
        @pl.when(group + distance < groups)
        def _():
            pl.semaphore_wait(ready.at[distance], size)
            for at in range(size):
                push((group + distance) * size + at)

    if s > 1:
        arrived(pair.at[pl.ds(0, s - 1)], pair_recv)
    total[...] = jnp.sum(pair[...], axis=0)
    for k in range(1, n):
        path = lax.rem(me + k, n)
        pltpu.make_async_remote_copy(
            src_ref=total,
            dst_ref=squares.at[me],
            send_sem=square_send,
            recv_sem=square_recv,
            device_id=device(path),
            device_id_type=MESH,
        ).start()
    squares[me] = total[...]

    limit = clip_ratio * math.sqrt(rows * s * width)
    own_shrink = jnp.minimum(1.0, limit / jnp.sqrt(total[...] + 1e-06))
    owner = [0 for _ in range(modules)]
    for path in range(n):
        for module in range(modules):
            owner[module] = jnp.where(module_ref[path] == module, path, owner[module])

    arrived(moments.at[pl.ds(0, n - 1)], moment_recv)
    for path in range(n):
        for low in range(0, columns, LANES):
            lanes = pl.ds(low, LANES)
            at = pl.ds(path * columns + low, LANES)
            clipped = own[:, at].astype(jnp.float32) * own_shrink
            moved = momentum_rate * moments[path, :, lanes] + clipped
            update[0, :, at] = (outer_rate * (clipped + momentum_rate * moved)).astype(jnp.bfloat16)

    arrived(squares.at[pl.ds(0, n - 1)], square_recv)
    shrink[...] = jnp.minimum(1.0, limit / jnp.sqrt(squares[...] + 1e-06))
    arrived(pieces.at[pl.ds(0, n - 1)], piece_recv)
    for module in range(modules):
        factor = shrink[owner[module]]
        piece = pieces[owner[module]].astype(jnp.float32)
        for low in range(0, columns, LANES):
            lanes = pl.ds(low, LANES)
            new[module, :, lanes] = (
                momentum_rate * momentum[module, :, lanes] + piece[:, low : low + LANES] * factor
            )

    arrived(pieces.at[pl.ds(0, n - 1)], piece_send)
    arrived(moments.at[pl.ds(0, n - 1)], moment_send)
    arrived(squares.at[pl.ds(0, n - 1)], square_send)
    if s > 1:
        arrived(pair.at[pl.ds(0, s - 1)], pair_send)


def write(update, new, update_ref, new_ref, sem):
    copies = [
        pltpu.make_async_copy(update, update_ref, sem.at[0]),
        pltpu.make_async_copy(new, new_ref, sem.at[1]),
    ]
    for copy in copies:
        copy.start()
    for copy in copies:
        copy.wait()


def direct(n, s, deltas, momentum, path_module):
    modules, rows, columns = momentum.shape
    width = deltas.shape[2]
    dma = pltpu.SemaphoreType.DMA
    regular = pltpu.SemaphoreType.REGULAR
    anywhere = pl.BlockSpec(memory_space=pl.ANY)
    in_vmem = pl.BlockSpec(memory_space=pltpu.VMEM)
    held = pl.pallas_call(
        functools.partial(kernel, n, s),
        out_shape=(
            pltpu.VMEM(deltas.shape, jnp.bfloat16),
            pltpu.VMEM(momentum.shape, jnp.float32),
        ),
        in_specs=[anywhere, anywhere, anywhere],
        out_specs=(in_vmem, in_vmem),
        scratch_shapes=[
            pltpu.SMEM(path_module.shape, jnp.int32),
            pltpu.VMEM((rows, width), jnp.bfloat16),
            pltpu.VMEM((modules, rows, columns), jnp.float32),
            pltpu.VMEM((n, rows, columns), jnp.float32),
            pltpu.VMEM((n, rows, columns), jnp.bfloat16),
            pltpu.VMEM((n, rows, columns), jnp.float32),
            pltpu.VMEM((1, LANES), jnp.float32),
            pltpu.VMEM((s, 1, LANES), jnp.float32),
            pltpu.VMEM((1, LANES), jnp.float32),
            pltpu.VMEM((n, 1, LANES), jnp.float32),
            pltpu.VMEM((n, 1, LANES), jnp.float32),
            dma((3,)),
            regular((n // math.gcd(n, 4),)),
            regular,
            dma,
            dma,
            dma,
            dma,
            dma,
            dma,
            dma,
            dma,
        ],
        compiler_params=pltpu.CompilerParams(collective_id=0, has_side_effects=True),
    )(deltas, momentum, path_module)
    return pl.pallas_call(
        write,
        out_shape=(
            jax.ShapeDtypeStruct(deltas.shape, jnp.bfloat16),
            jax.ShapeDtypeStruct(momentum.shape, jnp.float32),
        ),
        in_specs=[in_vmem, in_vmem],
        out_specs=(anywhere, anywhere),
        scratch_shapes=[dma((2,))],
    )(*[pltpu.with_memory_space_constraint(x, pltpu.VMEM) for x in held])


def by_collectives(s, deltas, momentum, path_module):
    modules = momentum.shape[0]
    rows, width = deltas.shape[1:]
    onehot = path_module[:, None] == jnp.arange(modules, dtype=jnp.int32)[None, :]
    counts = jnp.sum(onehot.astype(jnp.float32), axis=0)
    pieces = lax.all_to_all(deltas, "path", split_axis=2, concat_axis=0, tiled=True)
    totals = jnp.einsum(
        "pm,prc->mrc", onehot.astype(jnp.bfloat16), pieces, preferred_element_type=jnp.float32
    )
    outer_grad = totals / counts[:, None, None]
    local_squares = jnp.sum(outer_grad * outer_grad, axis=(1, 2))
    norm_squares = lax.psum(local_squares, ("path", "shard"))
    limit = clip_ratio * math.sqrt(rows * s * width)
    shrink = jnp.minimum(1.0, limit / jnp.sqrt(norm_squares + 1e-06))
    clipped = outer_grad * shrink[:, None, None]
    new_momentum = momentum_rate * momentum + clipped
    outer_step = (outer_rate * (clipped + momentum_rate * new_momentum)).astype(jnp.bfloat16)
    chosen = jnp.take(outer_step, path_module, axis=0)
    path_update = lax.all_to_all(chosen, "path", split_axis=0, concat_axis=2, tiled=True)
    return (path_update, new_momentum)


def local(n, s, deltas, momentum, path_module):
    modules, rows, columns = momentum.shape
    aligned = columns % LANES == 0 and rows % 16 == 0
    one_path_each = path_module.shape[0] == modules == n
    if aligned and one_path_each and n > 1:
        return direct(n, s, deltas, momentum, path_module)
    return by_collectives(s, deltas, momentum, path_module)


def solution(mesh):
    return jax.shard_map(
        functools.partial(local, mesh.shape["path"], mesh.shape["shard"]),
        mesh=mesh,
        in_specs=(P("path", "shard", None), P(None, "shard", "path"), P()),
        out_specs=(P("path", "shard", None), P(None, "shard", "path")),
        check_vma=False,
    )
```

time: 21.1 us -> 17.4 us (0.82)
  Pallas kernels: 20.3 us -> 16.6 us
    pallas_call x1, Pallas kernels: 19.6 us -> 15.8 us  [direct(): pl.pallas_call(functools.partial(kernel, n, s), out_shape=(pltpu.VMEM(del...]
where the time goes in v1:
time: 17.4 us; the launch traced here: 17.2 us
  Pallas kernels  16.6 us (95%)
  between operations  0.64 us (4%)
    pallas_call x1, Pallas kernels, direct(): pl.pallas_call(functools.partial(kernel, n, s), out_shape=(pltpu.VMEM(del...  15.8 us
    pallas_call x1, Pallas kernels, direct(): pl.pallas_call(write, out_shape=(jax.ShapeDtypeStruct(deltas.shape, jnp.b...  0.77 us

profile of v1, /device:TPU:0, one launch (start us, length us, event | category | flops | bytes accessed | tf_op | source)
XLA Modules:
  0.0 17.2 jit_solution(8922066946612087148)
XLA Ops:
  0.6 15.8 %shard_map.50 = (bf16[1,16,4096]{2,1,0:T(8,128)(2,1)S(1)}, f32[16,16,256]{2,1,0:T(8,128)S(1)}) custom-call(bf16[1,16,4096]{2,1,0:T(8,128)(2,1)} %deltas_ref.1, f32[16,16,256]{2,1,0:T(8,128)} %momentum_ref.1, s32[16]{0:T(128)} %path_module_ref.1), custom_call_target="tpu_custom_call" | custom-call | tf_op jit(solution)/shard_map/pallas_call | solution.py:223
  16.4 0.8 %shard_map.51 = (bf16[1,16,4096]{2,1,0:T(8,128)(2,1)}, f32[16,16,256]{2,1,0:T(8,128)}) custom-call(bf16[1,16,4096]{2,1,0:T(8,128)(2,1)S(1)} %get-tuple-element.4.update, f32[16,16,256]{2,1,0:T(8,128)S(1)} %get-tuple-element.5.new), custom_call_target="tpu_custom_call" | custom-call | tf_op jit(solution)/shard_map/pallas_call | solution.py:257

commit v2 on v1

v2 whole, which is shorter than its diff:
```python
import functools
import math

import jax
import jax.numpy as jnp
from jax import lax
from jax.experimental import pallas as pl
from jax.experimental.pallas import tpu as pltpu
from jax.sharding import PartitionSpec as P

outer_rate = 0.7
momentum_rate = 0.9
clip_ratio = 2.0
LANES = 128
MESH = pl.DeviceIdType.MESH


REACH = 2
REACH_FIRST = 2


def grid_of(n):
    cores = 2 if n % 2 == 0 else 1
    xs = 2 if n % 4 == 0 else 1
    return cores, xs, n // (cores * xs)


def when(condition, act):
    if condition is True:
        act()
    elif condition is not False:
        pl.when(condition)(act)


def opposite(condition):
    return not condition if isinstance(condition, bool) else jnp.logical_not(condition)


def kernel(
    n,
    s,
    deltas_ref,
    momentum_ref,
    path_module_ref,
    update,
    new,
    module_ref,
    own,
    momentum,
    chosen,
    pieces,
    moments,
    steps,
    mine,
    squares,
    shrink,
    load_sem,
    ready,
    cross,
    piece_send,
    piece_recv,
    moment_send,
    moment_recv,
    step_send,
    step_recv,
    square_send,
    square_recv,
):
    me, my_shard = lax.axis_index("path"), lax.axis_index("shard")
    modules, rows, columns = momentum.shape
    width = own.shape[1]
    cores, xs, slabs = grid_of(n)
    size = cores * xs
    core = lax.rem(me, cores)
    x = lax.rem(lax.div(me, cores), xs)
    slab = lax.div(me, size)
    limit = clip_ratio * math.sqrt(rows * s * width)
    first_shard, last_shard = my_shard == 0, my_shard == 1

    def arrived(buffer, sem):
        pltpu.make_async_copy(buffer, buffer, sem).wait()

    def signal(sem, path, shard=my_shard):
        pl.semaphore_signal(
            sem, inc=1, device_id={"path": path, "shard": shard}, device_id_type=MESH
        )

    def wait_for(sem, signals):
        when(signals > 0, lambda: pl.semaphore_wait(sem, signals))

    def block(index):
        return pl.ds(pl.multiple_of(index * columns, columns), columns)

    def send(source, target, send_sem, recv_sem, path, shard=my_shard):
        pltpu.make_async_remote_copy(
            src_ref=source,
            dst_ref=target,
            send_sem=send_sem,
            recv_sem=recv_sem,
            device_id={"path": path, "shard": shard},
            device_id_type=MESH,
        ).start()

    def push_piece(path):
        send(own.at[:, block(path)], pieces.at[me], piece_send, piece_recv.at[slab], path)

    def push_moment(path, distance):
        send(chosen.at[path], moments.at[me], moment_send.at[distance], moment_recv.at[distance], path)

    def push_square(path, shard=my_shard):
        kind = 0 if shard is my_shard else 1
        send(
            mine,
            squares.at[me, my_shard],
            square_send.at[kind],
            square_recv.at[kind * slabs + slab],
            path,
            shard,
        )

    def push_step(path, at_slab):
        send(
            steps.at[path],
            update.at[0, :, block(me)],
            step_send.at[at_slab],
            step_recv.at[slab],
            path,
        )

    def at(z, x_at, core_at):
        return z * size + x_at * cores + core_at

    def far(distance, path_slab):
        if distance >= REACH:
            return True
        if distance >= REACH_FIRST:
            return path_slab == 0
        return False

    def chip(act, z, x_at):
        for core_at in range(cores):
            act(at(z, x_at, core_at))

    def lower(condition, x_at, act):
        for distance in range(slabs - 1, 0, -1):
            def each():
                for core_at in range(cores):
                    act(at(slab - distance, x_at, core_at), distance)
            when((slab >= distance) & condition, each)

    def beside(act):
        for x_at in range(xs):
            for core_at in range(cores):
                behind = (x > x_at) | ((x == x_at) & (core > core_at))
                when(behind, lambda: act(at(slab, x_at, core_at)))

    def send_moment(path, distance):
        when(far(distance, slab - distance), lambda: push_moment(path, distance))

    barrier = pltpu.get_barrier_semaphore()
    for distance in range(slabs):
        for x_at in range(xs):
            inside = slab + distance < slabs
            if distance > 0:
                when(
                    inside & (x_at >= x),
                    lambda: chip(lambda path: signal(barrier, path), slab + distance, x_at),
                )
            else:
                for core_at in range(cores):
                    ahead = (x_at > x) | ((x_at == x) & (core_at > core))
                    when(ahead, lambda: signal(barrier, at(slab, x_at, core_at)))
            if s > 1:
                when(
                    inside & (x_at >= x) & first_shard,
                    lambda: chip(lambda path: signal(barrier, path, 1), slab + distance, x_at),
                )

    load_own = pltpu.make_async_copy(deltas_ref.at[0], own, load_sem.at[1])
    load_module = pltpu.make_async_copy(path_module_ref, module_ref, load_sem.at[0])
    load_momentum = pltpu.make_async_copy(momentum_ref, momentum, load_sem.at[2])
    load_own.start()
    load_module.start()
    load_momentum.start()

    before = (slab * (x + 1) + x) * cores + core
    wait_for(barrier, before + my_shard * (slab + 1) * (x + 1) * cores)
    for x_at in range(xs):
        lower(
            x >= x_at, x_at, lambda path, distance: signal(ready.at[distance * xs + x], path)
        )
    beside(lambda path: signal(ready.at[x], path))
    if s > 1:
        for x_at in range(xs):
            lower(
                last_shard & (x >= x_at),
                x_at,
                lambda path, distance: signal(cross.at[distance * xs + x], path, 0),
            )
            when(
                last_shard & (x >= x_at),
                lambda: chip(lambda path: signal(cross.at[x], path, 0), slab, x_at),
            )

    load_own.wait()
    held = own[...].astype(jnp.float32)
    by_column = jnp.sum(held * held, axis=0, keepdims=True)
    mine[...] = jnp.broadcast_to(jnp.sum(by_column, axis=1, keepdims=True), mine.shape)
    for x_at in range(xs):
        lower(x >= x_at, x_at, lambda path, distance: push_square(path))
        if s > 1:
            lower(
                last_shard & (x >= x_at), x_at, lambda path, distance: push_square(path, 0)
            )
            when(
                last_shard & (x >= x_at),
                lambda: chip(lambda path: push_square(path, 0), slab, x_at),
            )
    beside(push_square)
    for x_at in range(xs):
        lower(x >= x_at, x_at, lambda path, distance: push_piece(path))
    beside(push_piece)
    squares[me, my_shard] = mine[...]

    load_module.wait()
    load_momentum.wait()
    for distance in range(1, slabs):
        def choose():
            for b in range(size):
                path = (slab - distance) * size + b
                chosen[path] = momentum[module_ref[path]]
        if far(distance, slab - distance) is not False:
            when((slab >= distance) & far(distance, slab - distance), choose)
    pieces[me] = own[:, block(me)]

    if s > 1:
        def across():
            pl.semaphore_wait(cross.at[x], cores)
            for x_at in range(xs):
                lower(x >= x_at, x_at, lambda path, distance: push_square(path, 1))
                when(
                    x >= x_at,
                    lambda: chip(lambda path: push_square(path, 1), slab, x_at),
                )
        when(first_shard, across)

    for x_at in range(xs):
        def same_chip():
            wait_for(ready.at[x_at], cores - 1 - core)
            for core_at in range(1, cores):
                def give():
                    push_square(at(slab, x_at, core_at))
                    push_piece(at(slab, x_at, core_at))
                when(core_at > core, give)

        def next_chip():
            pl.semaphore_wait(ready.at[x_at], cores)
            lower(True, x_at, lambda path, distance: push_square(path))
            chip(push_square, slab, x_at)
            if s > 1:
                def over():
                    lower(True, x_at, lambda path, distance: push_square(path, 0))
                    chip(lambda path: push_square(path, 0), slab, x_at)
                when(last_shard, over)

            lower(True, x_at, lambda path, distance: push_piece(path))
            chip(push_piece, slab, x_at)

        when(x_at == x, same_chip)
        when(x_at > x, next_chip)

    if s > 1:
        for x_at in range(1, xs):
            def rest():
                pl.semaphore_wait(cross.at[x_at], cores)
                lower(True, x_at, lambda path, distance: push_square(path, 1))
                chip(lambda path: push_square(path, 1), slab, x_at)
            when((x_at > x) & first_shard, rest)

    def push_above(distance):
        def go():
            def give(x_at):
                chip(push_square, slab + distance, x_at)
                if s > 1:
                    when(
                        last_shard,
                        lambda: chip(lambda path: push_square(path, 0), slab + distance, x_at),
                    )
                chip(push_piece, slab + distance, x_at)

            for x_at in range(xs):
                def known():
                    pl.semaphore_wait(ready.at[distance * xs + x_at], cores)
                    give(x_at)
                when(x_at >= x, known)
                for low in range(x_at):
                    when(x_at == x, lambda: give(low))
        when(slab + distance < slabs, go)

    def cross_above(distance):
        def go():
            def give(x_at):
                chip(lambda path: push_square(path, 1), slab + distance, x_at)

            for x_at in range(xs):
                def known():
                    pl.semaphore_wait(cross.at[distance * xs + x_at], cores)
                    give(x_at)
                when(x_at >= x, known)
                for low in range(x_at):
                    when(x_at == x, lambda: give(low))
        when((slab + distance < slabs) & first_shard, go)

    for distance in range(1, slabs):
        push_above(distance)
        if s > 1:
            cross_above(distance)

    def step_of(clipped, previous):
        moved = momentum_rate * previous + clipped
        return (outer_rate * (clipped + momentum_rate * moved)).astype(jnp.bfloat16)

    def collect(source, count, answer):
        base = source * size
        arrived(pieces.at[pl.ds(0, count)], piece_recv.at[source])
        arrived(squares.at[pl.ds(0, count), 0], square_recv.at[source])
        if s > 1:
            arrived(squares.at[pl.ds(0, size), 0], square_recv.at[slabs + source])
        norm_squares = jnp.sum(squares[pl.ds(base, size)], axis=1)
        shrink[pl.ds(base, size)] = jnp.minimum(1.0, limit / jnp.sqrt(norm_squares + 1e-06))

        def reply():
            for b in range(size):
                module = module_ref[base + b]
                factor = shrink[base + b]
                for low in range(0, columns, LANES):
                    lanes = pl.ds(low, LANES)
                    clipped = pieces[base + b, :, lanes].astype(jnp.float32) * factor
                    steps[base + b, :, lanes] = step_of(clipped, momentum[module, :, lanes])
            for b in range(size):
                when(base + b != me, lambda: push_step(base + b, source))
        when(answer, reply)

    collect(slab, size - 1, True)
    for x_at in range(xs):
        lower(True, x_at, send_moment)

    update[0, :, block(me)] = steps[me]
    for distance in range(1, slabs):
        when(
            slab + distance < slabs,
            lambda: collect(slab + distance, size, True),
        )
        answer = opposite(far(distance, slab - distance))
        when(
            slab >= distance,
            lambda: collect(slab - distance, size, answer),
        )

    for distance in range(1, slabs):
        def receive():
            arrived(moments.at[pl.ds(0, size)], moment_recv.at[distance])
            factor = shrink[me]
            for b in range(size):
                owner = (slab + distance) * size + b
                for low in range(0, columns, LANES):
                    lanes = pl.ds(pl.multiple_of(owner * columns + low, LANES), LANES)
                    clipped = own[:, lanes].astype(jnp.float32) * factor
                    update[0, :, lanes] = step_of(clipped, moments[owner, :, pl.ds(low, LANES)])
        if far(distance, slab) is not False:
            when((slab + distance < slabs) & far(distance, slab), receive)

    source = [0 for _ in range(modules)]
    for path in range(n):
        for module in range(modules):
            source[module] = jnp.where(module_ref[path] == module, path, source[module])
    for module in range(modules):
        factor = shrink[source[module]]
        for low in range(0, columns, LANES):
            lanes = pl.ds(low, LANES)
            clipped = pieces[source[module], :, lanes].astype(jnp.float32) * factor
            new[module, :, lanes] = momentum_rate * momentum[module, :, lanes] + clipped

    arrived(pieces.at[pl.ds(0, n - 1)], piece_send)
    arrived(squares.at[pl.ds(0, n - 1), 0], square_send.at[0])
    if s > 1:
        arrived(squares.at[:, 0], square_send.at[1])
    arrived(steps.at[pl.ds(0, size - 1)], step_send.at[slab])
    for distance in range(1, slabs):
        above, below = slab + distance, slab - distance
        sent = far(distance, below)
        when(above < slabs, lambda: arrived(steps.at[pl.ds(0, size)], step_send.at[above]))
        if sent is not False:
            when(
                (below >= 0) & sent,
                lambda: arrived(moments.at[pl.ds(0, size)], moment_send.at[distance]),
            )
        if sent is not True:
            when(
                (below >= 0) & opposite(sent),
                lambda: arrived(steps.at[pl.ds(0, size)], step_send.at[below]),
            )
    arrived(steps.at[pl.ds(0, size - 1)], step_recv.at[slab])
    for distance in range(1, slabs):
        above, below = slab + distance, slab - distance
        got = far(distance, slab)
        when(below >= 0, lambda: arrived(steps.at[pl.ds(0, size)], step_recv.at[below]))
        if got is not True:
            when(
                (above < slabs) & opposite(got),
                lambda: arrived(steps.at[pl.ds(0, size)], step_recv.at[above]),
            )


def write(update, new, update_ref, new_ref, sem):
    copies = [
        pltpu.make_async_copy(update, update_ref, sem.at[0]),
        pltpu.make_async_copy(new, new_ref, sem.at[1]),
    ]
    for copy in copies:
        copy.start()
    for copy in copies:
        copy.wait()


def direct(n, s, deltas, momentum, path_module):
    modules, rows, columns = momentum.shape
    width = deltas.shape[2]
    _, xs, slabs = grid_of(n)
    dma = pltpu.SemaphoreType.DMA
    regular = pltpu.SemaphoreType.REGULAR
    anywhere = pl.BlockSpec(memory_space=pl.ANY)
    in_vmem = pl.BlockSpec(memory_space=pltpu.VMEM)
    held = pl.pallas_call(
        functools.partial(kernel, n, s),
        out_shape=(
            pltpu.VMEM(deltas.shape, jnp.bfloat16),
            pltpu.VMEM(momentum.shape, jnp.float32),
        ),
        in_specs=[anywhere, anywhere, anywhere],
        out_specs=(in_vmem, in_vmem),
        scratch_shapes=[
            pltpu.SMEM(path_module.shape, jnp.int32),
            pltpu.VMEM((rows, width), jnp.bfloat16),
            pltpu.VMEM((modules, rows, columns), jnp.float32),
            pltpu.VMEM((n, rows, columns), jnp.float32),
            pltpu.VMEM((n, rows, columns), jnp.bfloat16),
            pltpu.VMEM((n, rows, columns), jnp.float32),
            pltpu.VMEM((n, rows, columns), jnp.bfloat16),
            pltpu.VMEM((1, LANES), jnp.float32),
            pltpu.VMEM((n, s, 1, LANES), jnp.float32),
            pltpu.VMEM((n, 1, LANES), jnp.float32),
            dma((3,)),
            regular((slabs * xs,)),
            regular((slabs * xs,)),
            dma,
            dma((slabs,)),
            dma((slabs,)),
            dma((slabs,)),
            dma((slabs,)),
            dma((slabs,)),
            dma((2,)),
            dma((2 * slabs,)),
        ],
        compiler_params=pltpu.CompilerParams(collective_id=0, has_side_effects=True),
    )(deltas, momentum, path_module)
    return pl.pallas_call(
        write,
        out_shape=(
            jax.ShapeDtypeStruct(deltas.shape, jnp.bfloat16),
            jax.ShapeDtypeStruct(momentum.shape, jnp.float32),
        ),
        in_specs=[in_vmem, in_vmem],
        out_specs=(anywhere, anywhere),
        scratch_shapes=[dma((2,))],
    )(*[pltpu.with_memory_space_constraint(x, pltpu.VMEM) for x in held])


def by_collectives(s, deltas, momentum, path_module):
    modules = momentum.shape[0]
    rows, width = deltas.shape[1:]
    onehot = path_module[:, None] == jnp.arange(modules, dtype=jnp.int32)[None, :]
    counts = jnp.sum(onehot.astype(jnp.float32), axis=0)
    pieces = lax.all_to_all(deltas, "path", split_axis=2, concat_axis=0, tiled=True)
    totals = jnp.einsum(
        "pm,prc->mrc", onehot.astype(jnp.bfloat16), pieces, preferred_element_type=jnp.float32
    )
    outer_grad = totals / counts[:, None, None]
    local_squares = jnp.sum(outer_grad * outer_grad, axis=(1, 2))
    norm_squares = lax.psum(local_squares, ("path", "shard"))
    limit = clip_ratio * math.sqrt(rows * s * width)
    shrink = jnp.minimum(1.0, limit / jnp.sqrt(norm_squares + 1e-06))
    clipped = outer_grad * shrink[:, None, None]
    new_momentum = momentum_rate * momentum + clipped
    outer_step = (outer_rate * (clipped + momentum_rate * new_momentum)).astype(jnp.bfloat16)
    chosen = jnp.take(outer_step, path_module, axis=0)
    path_update = lax.all_to_all(chosen, "path", split_axis=0, concat_axis=2, tiled=True)
    return (path_update, new_momentum)


def local(n, s, deltas, momentum, path_module):
    modules, rows, columns = momentum.shape
    aligned = columns % LANES == 0 and rows % 16 == 0
    one_path_each = path_module.shape[0] == modules == n
    if aligned and one_path_each and n > 1 and s <= 2:
        return direct(n, s, deltas, momentum, path_module)
    return by_collectives(s, deltas, momentum, path_module)


def solution(mesh):
    return jax.shard_map(
        functools.partial(local, mesh.shape["path"], mesh.shape["shard"]),
        mesh=mesh,
        in_specs=(P("path", "shard", None), P(None, "shard", "path"), P()),
        out_specs=(P("path", "shard", None), P(None, "shard", "path")),
        check_vma=False,
    )
```

time: 17.4 us -> 15.6 us (0.90)
  the two profiles are of different devices: /device:TPU:0 before, /device:TPU:9 now
where the time goes in v2:
time: 15.6 us; the launch traced here: 15.5 us
  Pallas kernels  14.9 us (96%)
  between operations  0.64 us (4%)
    pallas_call x1, Pallas kernels, direct(): pl.pallas_call(functools.partial(kernel, n, s), out_shape=(pltpu.VMEM(del...  14.1 us
    pallas_call x1, Pallas kernels, direct(): pl.pallas_call(write, out_shape=(jax.ShapeDtypeStruct(deltas.shape, jnp.b...  0.77 us

profile of v2, /device:TPU:9, one launch (start us, length us, event | category | flops | bytes accessed | tf_op | source)
XLA Modules:
  0.0 15.5 jit_solution(14168099248791661007)
XLA Ops:
  0.6 14.1 %shard_map.50 = (bf16[1,16,4096]{2,1,0:T(8,128)(2,1)S(1)}, f32[16,16,256]{2,1,0:T(8,128)S(1)}) custom-call(bf16[1,16,4096]{2,1,0:T(8,128)(2,1)} %deltas_ref.1, f32[16,16,256]{2,1,0:T(8,128)} %momentum_ref.1, s32[16]{0:T(128)} %path_module_ref.1), custom_call_target="tpu_custom_call" | custom-call | tf_op jit(solution)/shard_map/pallas_call | solution.py:434
  14.7 0.8 %shard_map.51 = (bf16[1,16,4096]{2,1,0:T(8,128)(2,1)}, f32[16,16,256]{2,1,0:T(8,128)}) custom-call(bf16[1,16,4096]{2,1,0:T(8,128)(2,1)S(1)} %get-tuple-element.4.update, f32[16,16,256]{2,1,0:T(8,128)S(1)} %get-tuple-element.5.new), custom_call_target="tpu_custom_call" | custom-call | tf_op jit(solution)/shard_map/pallas_call | solution.py:467

commit v3 on v2

--- a/solution.py
+++ b/solution.py
@@ -15,7 +15,7 @@
 MESH = pl.DeviceIdType.MESH
 
 
-REACH = 2
+REACH = 3
 REACH_FIRST = 2
 
 
@@ -30,6 +30,10 @@
         act()
     elif condition is not False:
         pl.when(condition)(act)
+
+
+def tally_rows(rows, columns):
+    return rows * columns * 2 // (LANES * 4), rows * columns * 4 // (LANES * 4)
 
 
 def opposite(condition):
@@ -54,17 +58,14 @@
     mine,
     squares,
     shrink,
+    tally,
     load_sem,
     ready,
     cross,
-    piece_send,
-    piece_recv,
-    moment_send,
-    moment_recv,
-    step_send,
-    step_recv,
-    square_send,
-    square_recv,
+    left,
+    came,
+    moment_came,
+    step_came,
 ):
     me, my_shard = lax.axis_index("path"), lax.axis_index("shard")
     modules, rows, columns = momentum.shape
@@ -75,10 +76,13 @@
     x = lax.rem(lax.div(me, cores), xs)
     slab = lax.div(me, size)
     limit = clip_ratio * math.sqrt(rows * s * width)
+    piece_rows, moment_rows = tally_rows(rows, columns)
     first_shard, last_shard = my_shard == 0, my_shard == 1
 
-    def arrived(buffer, sem):
-        pltpu.make_async_copy(buffer, buffer, sem).wait()
+    def arrived(count, sem):
+        if count > 0:
+            part = tally.at[pl.ds(0, count)]
+            pltpu.make_async_copy(part, part, sem).wait()
 
     def signal(sem, path, shard=my_shard):
         pl.semaphore_signal(
@@ -91,41 +95,27 @@
     def block(index):
         return pl.ds(pl.multiple_of(index * columns, columns), columns)
 
-    def send(source, target, send_sem, recv_sem, path, shard=my_shard):
+    def send(source, target, recv_sem, path, shard=my_shard):
         pltpu.make_async_remote_copy(
             src_ref=source,
             dst_ref=target,
-            send_sem=send_sem,
+            send_sem=left,
             recv_sem=recv_sem,
             device_id={"path": path, "shard": shard},
             device_id_type=MESH,
         ).start()
 
     def push_piece(path):
-        send(own.at[:, block(path)], pieces.at[me], piece_send, piece_recv.at[slab], path)
+        send(own.at[:, block(path)], pieces.at[me], came.at[slab], path)
 
     def push_moment(path, distance):
-        send(chosen.at[path], moments.at[me], moment_send.at[distance], moment_recv.at[distance], path)
+        send(chosen.at[path], moments.at[me], moment_came, path)
 
     def push_square(path, shard=my_shard):
-        kind = 0 if shard is my_shard else 1
-        send(
-            mine,
-            squares.at[me, my_shard],
-            square_send.at[kind],
-            square_recv.at[kind * slabs + slab],
-            path,
-            shard,
-        )
-
-    def push_step(path, at_slab):
-        send(
-            steps.at[path],
-            update.at[0, :, block(me)],
-            step_send.at[at_slab],
-            step_recv.at[slab],
-            path,
-        )
+        send(mine, squares.at[me * s + my_shard], came.at[slab], path, shard)
+
+    def push_step(path):
+        send(steps.at[path], update.at[0, :, block(me)], step_came, path)
 
     def at(z, x_at, core_at):
         return z * size + x_at * cores + core_at
@@ -156,6 +146,13 @@
 
     def send_moment(path, distance):
         when(far(distance, slab - distance), lambda: push_moment(path, distance))
+
+    load_own = pltpu.make_async_copy(deltas_ref.at[0], own, load_sem.at[1])
+    load_module = pltpu.make_async_copy(path_module_ref, module_ref, load_sem.at[0])
+    load_momentum = pltpu.make_async_copy(momentum_ref, momentum, load_sem.at[2])
+    load_own.start()
+    load_module.start()
+    load_momentum.start()
 
     barrier = pltpu.get_barrier_semaphore()
     for distance in range(slabs):
@@ -176,13 +173,6 @@
                     lambda: chip(lambda path: signal(barrier, path, 1), slab + distance, x_at),
                 )
 
-    load_own = pltpu.make_async_copy(deltas_ref.at[0], own, load_sem.at[1])
-    load_module = pltpu.make_async_copy(path_module_ref, module_ref, load_sem.at[0])
-    load_momentum = pltpu.make_async_copy(momentum_ref, momentum, load_sem.at[2])
-    load_own.start()
-    load_module.start()
-    load_momentum.start()
-
     before = (slab * (x + 1) + x) * cores + core
     wait_for(barrier, before + my_shard * (slab + 1) * (x + 1) * cores)
     for x_at in range(xs):
@@ -220,7 +210,7 @@
     for x_at in range(xs):
         lower(x >= x_at, x_at, lambda path, distance: push_piece(path))
     beside(push_piece)
-    squares[me, my_shard] = mine[...]
+    squares[me * s + my_shard] = mine[...]
 
     load_module.wait()
     load_momentum.wait()
@@ -316,17 +306,18 @@
         if s > 1:
             cross_above(distance)
 
+    for x_at in range(xs):
+        lower(True, x_at, lambda path, distance: send_moment(path, distance) if distance in (3,) else None)
+
     def step_of(clipped, previous):
         moved = momentum_rate * previous + clipped
         return (outer_rate * (clipped + momentum_rate * moved)).astype(jnp.bfloat16)
 
     def collect(source, count, answer):
         base = source * size
-        arrived(pieces.at[pl.ds(0, count)], piece_recv.at[source])
-        arrived(squares.at[pl.ds(0, count), 0], square_recv.at[source])
-        if s > 1:
-            arrived(squares.at[pl.ds(0, size), 0], square_recv.at[slabs + source])
-        norm_squares = jnp.sum(squares[pl.ds(base, size)], axis=1)
+        arrived(count * piece_rows + count * s + (size - count) * (s - 1), came.at[source])
+        both = squares[pl.ds(base * s, size * s)].reshape(size, s, 1, LANES)
+        norm_squares = jnp.sum(both, axis=1)
         shrink[pl.ds(base, size)] = jnp.minimum(1.0, limit / jnp.sqrt(norm_squares + 1e-06))
 
         def reply():
@@ -338,37 +329,25 @@
                     clipped = pieces[base + b, :, lanes].astype(jnp.float32) * factor
                     steps[base + b, :, lanes] = step_of(clipped, momentum[module, :, lanes])
             for b in range(size):
-                when(base + b != me, lambda: push_step(base + b, source))
+                when(base + b != me, lambda: push_step(base + b))
         when(answer, reply)
 
     collect(slab, size - 1, True)
     for x_at in range(xs):
-        lower(True, x_at, send_moment)
+        lower(True, x_at, lambda path, distance: send_moment(path, distance) if distance in (1, 2) else None)
 
     update[0, :, block(me)] = steps[me]
+    for distance in range(1, slabs):
+        answer = opposite(far(distance, slab - distance))
+        when(
+            slab >= distance,
+            lambda: collect(slab - distance, size, answer),
+        )
     for distance in range(1, slabs):
         when(
             slab + distance < slabs,
             lambda: collect(slab + distance, size, True),
         )
-        answer = opposite(far(distance, slab - distance))
-        when(
-            slab >= distance,
-            lambda: collect(slab - distance, size, answer),
-        )
-
-    for distance in range(1, slabs):
-        def receive():
-            arrived(moments.at[pl.ds(0, size)], moment_recv.at[distance])
-            factor = shrink[me]
-            for b in range(size):
-                owner = (slab + distance) * size + b
-                for low in range(0, columns, LANES):
-                    lanes = pl.ds(pl.multiple_of(owner * columns + low, LANES), LANES)
-                    clipped = own[:, lanes].astype(jnp.float32) * factor
-                    update[0, :, lanes] = step_of(clipped, moments[owner, :, pl.ds(low, LANES)])
-        if far(distance, slab) is not False:
-            when((slab + distance < slabs) & far(distance, slab), receive)
 
     source = [0 for _ in range(modules)]
     for path in range(n):
@@ -381,35 +360,23 @@
             clipped = pieces[source[module], :, lanes].astype(jnp.float32) * factor
             new[module, :, lanes] = momentum_rate * momentum[module, :, lanes] + clipped
 
-    arrived(pieces.at[pl.ds(0, n - 1)], piece_send)
-    arrived(squares.at[pl.ds(0, n - 1), 0], square_send.at[0])
-    if s > 1:
-        arrived(squares.at[:, 0], square_send.at[1])
-    arrived(steps.at[pl.ds(0, size - 1)], step_send.at[slab])
-    for distance in range(1, slabs):
-        above, below = slab + distance, slab - distance
-        sent = far(distance, below)
-        when(above < slabs, lambda: arrived(steps.at[pl.ds(0, size)], step_send.at[above]))
-        if sent is not False:
-            when(
-                (below >= 0) & sent,
-                lambda: arrived(moments.at[pl.ds(0, size)], moment_send.at[distance]),
-            )
-        if sent is not True:
-            when(
-                (below >= 0) & opposite(sent),
-                lambda: arrived(steps.at[pl.ds(0, size)], step_send.at[below]),
-            )
-    arrived(steps.at[pl.ds(0, size - 1)], step_recv.at[slab])
-    for distance in range(1, slabs):
-        above, below = slab + distance, slab - distance
-        got = far(distance, slab)
-        when(below >= 0, lambda: arrived(steps.at[pl.ds(0, size)], step_recv.at[below]))
-        if got is not True:
-            when(
-                (above < slabs) & opposite(got),
-                lambda: arrived(steps.at[pl.ds(0, size)], step_recv.at[above]),
-            )
+    def finish(at_slab):
+        owners = [z for z in range(at_slab + 1, slabs) if far(z - at_slab, at_slab)]
+        arrived(len(owners) * size * moment_rows, moment_came)
+        factor = shrink[me]
+        for owner in [z * size + b for z in owners for b in range(size)]:
+            for low in range(0, columns, LANES):
+                lanes = pl.ds(owner * columns + low, LANES)
+                clipped = own[:, lanes].astype(jnp.float32) * factor
+                update[0, :, lanes] = step_of(clipped, moments[owner, :, pl.ds(low, LANES)])
+        told = [z for z in range(at_slab) if far(at_slab - z, z)]
+        sent = (n - 1) * piece_rows + n * s - 1 + len(told) * size * moment_rows
+        sent += ((slabs - len(told)) * size - 1) * piece_rows
+        arrived(sent, left)
+        arrived(((slabs - len(owners)) * size - 1) * piece_rows, step_came)
+
+    for at_slab in range(slabs):
+        when(slab == at_slab, lambda: finish(at_slab))
 
 
 def write(update, new, update_ref, new_ref, sem):
@@ -427,6 +394,7 @@
     modules, rows, columns = momentum.shape
     width = deltas.shape[2]
     _, xs, slabs = grid_of(n)
+    piece_rows, moment_rows = tally_rows(rows, columns)
     dma = pltpu.SemaphoreType.DMA
     regular = pltpu.SemaphoreType.REGULAR
     anywhere = pl.BlockSpec(memory_space=pl.ANY)
@@ -448,19 +416,16 @@
             pltpu.VMEM((n, rows, columns), jnp.float32),
             pltpu.VMEM((n, rows, columns), jnp.bfloat16),
             pltpu.VMEM((1, LANES), jnp.float32),
-            pltpu.VMEM((n, s, 1, LANES), jnp.float32),
+            pltpu.VMEM((n * s, 1, LANES), jnp.float32),
             pltpu.VMEM((n, 1, LANES), jnp.float32),
+            pltpu.VMEM((n * (2 * piece_rows + moment_rows + s), 1, LANES), jnp.float32),
             dma((3,)),
             regular((slabs * xs,)),
             regular((slabs * xs,)),
             dma,
             dma((slabs,)),
-            dma((slabs,)),
-            dma((slabs,)),
-            dma((slabs,)),
-            dma((slabs,)),
-            dma((2,)),
-            dma((2 * slabs,)),
+            dma,
+            dma,
         ],
         compiler_params=pltpu.CompilerParams(collective_id=0, has_side_effects=True),
     )(deltas, momentum, path_module)

time: 15.6 us -> 15 us (0.962)
  the two profiles are of different devices: /device:TPU:9 before, /device:TPU:0 now
where the time goes in v3:
time: 15 us; the launch traced here: 14.8 us
  Pallas kernels  14.2 us (95%)
  between operations  0.64 us (4%)
    pallas_call x1, Pallas kernels, direct(): pl.pallas_call(functools.partial(kernel, n, s), out_shape=(pltpu.VMEM(del...  13.4 us
    pallas_call x1, Pallas kernels, direct(): pl.pallas_call(write, out_shape=(jax.ShapeDtypeStruct(deltas.shape, jnp.b...  0.77 us

profile of v3, /device:TPU:0, one launch (start us, length us, event | category | flops | bytes accessed | tf_op | source)
XLA Modules:
  0.0 14.8 jit_solution(16141058886199422104)
XLA Ops:
  0.6 13.4 %shard_map.50 = (bf16[1,16,4096]{2,1,0:T(8,128)(2,1)S(1)}, f32[16,16,256]{2,1,0:T(8,128)S(1)}) custom-call(bf16[1,16,4096]{2,1,0:T(8,128)(2,1)} %deltas_ref.1, f32[16,16,256]{2,1,0:T(8,128)} %momentum_ref.1, s32[16]{0:T(128)} %path_module_ref.1), custom_call_target="tpu_custom_call" | custom-call | tf_op jit(solution)/shard_map/pallas_call | solution.py:402
  14.0 0.8 %shard_map.51 = (bf16[1,16,4096]{2,1,0:T(8,128)(2,1)}, f32[16,16,256]{2,1,0:T(8,128)}) custom-call(bf16[1,16,4096]{2,1,0:T(8,128)(2,1)S(1)} %get-tuple-element.4.update, f32[16,16,256]{2,1,0:T(8,128)S(1)} %get-tuple-element.5.new), custom_call_target="tpu_custom_call" | custom-call | tf_op jit(solution)/shard_map/pallas_call | solution.py:432

commit v4 on v3

--- a/solution.py
+++ b/solution.py
@@ -15,8 +15,8 @@
 MESH = pl.DeviceIdType.MESH
 
 
-REACH = 3
-REACH_FIRST = 2
+REACH = 2
+REACH_FIRST = 1
 
 
 def grid_of(n):
@@ -185,7 +185,7 @@
             lower(
                 last_shard & (x >= x_at),
                 x_at,
-                lambda path, distance: signal(cross.at[distance * xs + x], path, 0),
+                lambda path, distance: signal(cross.at[xs - 1 + distance], path, 0),
             )
             when(
                 last_shard & (x >= x_at),
@@ -221,6 +221,12 @@
                 chosen[path] = momentum[module_ref[path]]
         if far(distance, slab - distance) is not False:
             when((slab >= distance) & far(distance, slab - distance), choose)
+    for x_at in range(xs):
+        lower(
+            x >= x_at,
+            x_at,
+            lambda path, distance: send_moment(path, distance) if distance in (1,) else None,
+        )
     pieces[me] = own[:, block(me)]
 
     if s > 1:
@@ -254,18 +260,15 @@
                 when(last_shard, over)
 
             lower(True, x_at, lambda path, distance: push_piece(path))
+            lower(
+                True,
+                x_at,
+                lambda path, distance: send_moment(path, distance) if distance in (1,) else None,
+            )
             chip(push_piece, slab, x_at)
 
         when(x_at == x, same_chip)
         when(x_at > x, next_chip)
-
-    if s > 1:
-        for x_at in range(1, xs):
-            def rest():
-                pl.semaphore_wait(cross.at[x_at], cores)
-                lower(True, x_at, lambda path, distance: push_square(path, 1))
-                chip(lambda path: push_square(path, 1), slab, x_at)
-            when((x_at > x) & first_shard, rest)
 
     def push_above(distance):
         def go():
@@ -292,19 +295,31 @@
             def give(x_at):
                 chip(lambda path: push_square(path, 1), slab + distance, x_at)
 
+            pl.semaphore_wait(cross.at[xs - 1 + distance], (xs - x) * cores)
             for x_at in range(xs):
-                def known():
-                    pl.semaphore_wait(cross.at[distance * xs + x_at], cores)
-                    give(x_at)
-                when(x_at >= x, known)
-                for low in range(x_at):
-                    when(x_at == x, lambda: give(low))
+                give(x_at)
         when((slab + distance < slabs) & first_shard, go)
 
-    for distance in range(1, slabs):
-        push_above(distance)
-        if s > 1:
-            cross_above(distance)
+    if slabs > 1:
+        push_above(1)
+    if s > 1:
+        for x_at in range(1, xs):
+            def rest():
+                pl.semaphore_wait(cross.at[x_at], cores)
+                lower(True, x_at, lambda path, distance: push_square(path, 1))
+                chip(lambda path: push_square(path, 1), slab, x_at)
+            when((x_at > x) & first_shard, rest)
+
+    if slabs > 2:
+        push_above(2)
+    if s > 1 and slabs > 1:
+        cross_above(1)
+    if slabs > 3:
+        push_above(3)
+    if s > 1 and slabs > 2:
+        cross_above(2)
+    if s > 1 and slabs > 3:
+        cross_above(3)
 
     for x_at in range(xs):
         lower(True, x_at, lambda path, distance: send_moment(path, distance) if distance in (3,) else None)
@@ -334,7 +349,7 @@
 
     collect(slab, size - 1, True)
     for x_at in range(xs):
-        lower(True, x_at, lambda path, distance: send_moment(path, distance) if distance in (1, 2) else None)
+        lower(True, x_at, lambda path, distance: send_moment(path, distance) if distance in (2,) else None)
 
     update[0, :, block(me)] = steps[me]
     for distance in range(1, slabs):
@@ -421,7 +436,7 @@
             pltpu.VMEM((n * (2 * piece_rows + moment_rows + s), 1, LANES), jnp.float32),
             dma((3,)),
             regular((slabs * xs,)),
-            regular((slabs * xs,)),
+            regular((xs + slabs - 1,)),
             dma,
             dma((slabs,)),
             dma,

time: 15 us -> 14.7 us (0.980)
  the two profiles are of different devices: /device:TPU:0 before, /device:TPU:29 now
where the time goes in v4:
time: 14.7 us; the launch traced here: 14.6 us
  Pallas kernels  13.9 us (95%)
  between operations  0.64 us (4%)
    pallas_call x1, Pallas kernels, direct(): pl.pallas_call(functools.partial(kernel, n, s), out_shape=(pltpu.VMEM(del...  13.2 us
    pallas_call x1, Pallas kernels, direct(): pl.pallas_call(write, out_shape=(jax.ShapeDtypeStruct(deltas.shape, jnp.b...  0.77 us

profile of v4, /device:TPU:29, one launch (start us, length us, event | category | flops | bytes accessed | tf_op | source)
XLA Modules:
  0.0 14.6 jit_solution(6618330018376231404)
XLA Ops:
  0.6 13.2 %shard_map.50 = (bf16[1,16,4096]{2,1,0:T(8,128)(2,1)S(1)}, f32[16,16,256]{2,1,0:T(8,128)S(1)}) custom-call(bf16[1,16,4096]{2,1,0:T(8,128)(2,1)} %deltas_ref.1, f32[16,16,256]{2,1,0:T(8,128)} %momentum_ref.1, s32[16]{0:T(128)} %path_module_ref.1), custom_call_target="tpu_custom_call" | custom-call | tf_op jit(solution)/shard_map/pallas_call | solution.py:417
  13.8 0.8 %shard_map.51 = (bf16[1,16,4096]{2,1,0:T(8,128)(2,1)}, f32[16,16,256]{2,1,0:T(8,128)}) custom-call(bf16[1,16,4096]{2,1,0:T(8,128)(2,1)S(1)} %get-tuple-element.4.update, f32[16,16,256]{2,1,0:T(8,128)S(1)} %get-tuple-element.5.new), custom_call_target="tpu_custom_call" | custom-call | tf_op jit(solution)/shard_map/pallas_call | solution.py:447

commit v5 on v4

--- a/solution.py
+++ b/solution.py
@@ -193,9 +193,15 @@
             )
 
     load_own.wait()
-    held = own[...].astype(jnp.float32)
-    by_column = jnp.sum(held * held, axis=0, keepdims=True)
-    mine[...] = jnp.broadcast_to(jnp.sum(by_column, axis=1, keepdims=True), mine.shape)
+    parts = []
+    for low in range(0, width, LANES):
+        held = own[:, low : low + LANES].astype(jnp.float32)
+        parts.append(held * held)
+    while len(parts) > 1:
+        odd = parts[len(parts) // 2 * 2 :]
+        parts = [a + b for a, b in zip(parts[0::2], parts[1::2])] + odd
+    by_lane = jnp.sum(parts[0], axis=0, keepdims=True)
+    mine[...] = jnp.broadcast_to(jnp.sum(by_lane, axis=1, keepdims=True), mine.shape)
     for x_at in range(xs):
         lower(x >= x_at, x_at, lambda path, distance: push_square(path))
         if s > 1:
@@ -207,7 +213,7 @@
                 lambda: chip(lambda path: push_square(path, 0), slab, x_at),
             )
     beside(push_square)
-    for x_at in range(xs):
+    for x_at in reversed(range(xs)):
         lower(x >= x_at, x_at, lambda path, distance: push_piece(path))
     beside(push_piece)
     squares[me * s + my_shard] = mine[...]

time: 14.7 us -> 14.7 us (level)
  the two profiles are of different devices: /device:TPU:29 before, /device:TPU:0 now
where the time goes in v5:
time: 14.7 us; the launch traced here: 14.5 us
  Pallas kernels  13.8 us (94%)
  between operations  0.64 us (4%)
    pallas_call x1, Pallas kernels, direct(): pl.pallas_call(functools.partial(kernel, n, s), out_shape=(pltpu.VMEM(del...  13 us
    pallas_call x1, Pallas kernels, direct(): pl.pallas_call(write, out_shape=(jax.ShapeDtypeStruct(deltas.shape, jnp.b...  0.77 us

profile of v5, /device:TPU:0, one launch (start us, length us, event | category | flops | bytes accessed | tf_op | source)
XLA Modules:
  0.0 14.5 jit_solution(7731735477333529261)
XLA Ops:
  0.6 13.0 %shard_map.50 = (bf16[1,16,4096]{2,1,0:T(8,128)(2,1)S(1)}, f32[16,16,256]{2,1,0:T(8,128)S(1)}) custom-call(bf16[1,16,4096]{2,1,0:T(8,128)(2,1)} %deltas_ref.1, f32[16,16,256]{2,1,0:T(8,128)} %momentum_ref.1, s32[16]{0:T(128)} %path_module_ref.1), custom_call_target="tpu_custom_call" | custom-call | tf_op jit(solution)/shard_map/pallas_call | solution.py:423
  13.7 0.8 %shard_map.51 = (bf16[1,16,4096]{2,1,0:T(8,128)(2,1)}, f32[16,16,256]{2,1,0:T(8,128)}) custom-call(bf16[1,16,4096]{2,1,0:T(8,128)(2,1)S(1)} %get-tuple-element.4.update, f32[16,16,256]{2,1,0:T(8,128)S(1)} %get-tuple-element.5.new), custom_call_target="tpu_custom_call" | custom-call | tf_op jit(solution)/shard_map/pallas_call | solution.py:453

commit v6 on v5

--- a/solution.py
+++ b/solution.py
@@ -175,11 +175,6 @@
 
     before = (slab * (x + 1) + x) * cores + core
     wait_for(barrier, before + my_shard * (slab + 1) * (x + 1) * cores)
-    for x_at in range(xs):
-        lower(
-            x >= x_at, x_at, lambda path, distance: signal(ready.at[distance * xs + x], path)
-        )
-    beside(lambda path: signal(ready.at[x], path))
     if s > 1:
         for x_at in range(xs):
             lower(
@@ -191,6 +186,11 @@
                 last_shard & (x >= x_at),
                 lambda: chip(lambda path: signal(cross.at[x], path, 0), slab, x_at),
             )
+    for x_at in range(xs):
+        lower(
+            x >= x_at, x_at, lambda path, distance: signal(ready.at[distance * xs + x], path)
+        )
+    beside(lambda path: signal(ready.at[x], path))
 
     load_own.wait()
     parts = []

time: 14.7 us -> 14.7 us (level)
  no operation moved by 1% of the time
where the time goes in v6:
time: 14.7 us; the launch traced here: 14.5 us
  Pallas kernels  13.8 us (94%)
  between operations  0.64 us (4%)
    pallas_call x1, Pallas kernels, direct(): pl.pallas_call(functools.partial(kernel, n, s), out_shape=(pltpu.VMEM(del...  13.1 us
    pallas_call x1, Pallas kernels, direct(): pl.pallas_call(write, out_shape=(jax.ShapeDtypeStruct(deltas.shape, jnp.b...  0.77 us

profile of v6, /device:TPU:0, one launch (start us, length us, event | category | flops | bytes accessed | tf_op | source)
XLA Modules:
  0.0 14.5 jit_solution(4235390097295730744)
XLA Ops:
  0.6 13.1 %shard_map.50 = (bf16[1,16,4096]{2,1,0:T(8,128)(2,1)S(1)}, f32[16,16,256]{2,1,0:T(8,128)S(1)}) custom-call(bf16[1,16,4096]{2,1,0:T(8,128)(2,1)} %deltas_ref.1, f32[16,16,256]{2,1,0:T(8,128)} %momentum_ref.1, s32[16]{0:T(128)} %path_module_ref.1), custom_call_target="tpu_custom_call" | custom-call | tf_op jit(solution)/shard_map/pallas_call | solution.py:423
  13.7 0.8 %shard_map.51 = (bf16[1,16,4096]{2,1,0:T(8,128)(2,1)}, f32[16,16,256]{2,1,0:T(8,128)}) custom-call(bf16[1,16,4096]{2,1,0:T(8,128)(2,1)S(1)} %get-tuple-element.4.update, f32[16,16,256]{2,1,0:T(8,128)S(1)} %get-tuple-element.5.new), custom_call_target="tpu_custom_call" | custom-call | tf_op jit(solution)/shard_map/pallas_call | solution.py:453
